TPU v7x, 32 devices: a whole 2x2x4 slice. The times are simulated.
32 devices in a mesh: row: 4 (over x, core), col: 8 (over z, y).
Axes of the slice: x: 2, y: 2, z: 4, core: 2. Of those that a mesh axis runs over, the one named last changes fastest.
Arguments:
- stem: float32 [2, 4, 1024, 1024], P(None, 'row', 'col'), may hold values from -6 to 6
- branch: float32 [2, 1024, 1024], replicated, may hold values from -0.125 to 0.125
Outputs:
- absorbed: float32 [2, 1024, 4, 1024], P(None, ('row', 'col'))
All inputs are finite; a program needn't handle non-finite values.
Results may differ from a plain program's by a relative error of at most 0.00007.
Values sent between devices are 32-bit elements; how exact they have to be, the bound alone decides.
No kernel may reach another device: no remote copies, remote signals or barrier semaphores. Data moves between devices by JAX's collectives and lax.ppermute only.
A program may use at most 64 MiB of HBM per device.

v0:
```python
import jax
import jax.numpy as jnp
from jax import lax
from jax.sharding import PartitionSpec as P


def per_device(stem, branch):
    rows_count = lax.axis_size("row")
    cols_count = lax.axis_size("col")
    entries = stem.shape[2]
    remain = stem.shape[3]
    contract = branch.shape[1]
    opened = branch.shape[2]
    whole_b = entries * cols_count
    middle = whole_b // contract
    blocks = stem.reshape(
        2, 1, entries, rows_count, cols_count, remain // (rows_count * cols_count)
    )
    moved = lax.all_to_all(blocks, "col", split_axis=4, concat_axis=2, tiled=True)
    moved = lax.all_to_all(moved, "row", split_axis=3, concat_axis=1, tiled=True)
    owned = remain // (rows_count * cols_count)
    split = moved.reshape(2, rows_count, contract, middle, owned)
    high = lax.Precision.HIGHEST
    real = jnp.einsum("akml,ko->lamo", split[0], branch[0], precision=high) - jnp.einsum(
        "akml,ko->lamo", split[1], branch[1], precision=high
    )
    imag = jnp.einsum("akml,ko->lamo", split[0], branch[1], precision=high) + jnp.einsum(
        "akml,ko->lamo", split[1], branch[0], precision=high
    )
    joined = jnp.stack([real, imag])
    return joined.reshape(2, owned, rows_count, middle * opened)


def solution(mesh):
    placed = (P(None, "row", "col", None), P())
    return jax.shard_map(
        per_device,
        mesh=mesh,
        in_specs=placed,
        out_specs=P(None, ("row", "col"), None, None),
        check_vma=False,
    )
```

profile of v0, /device:TPU:0, one launch (start us, length us, event | category | flops | bytes accessed | tf_op | source)
XLA Modules:
  0.0 64.5 jit_solution(6183118400179936068)
XLA Ops:
  0.0 1.5 %copy.12 = f32[2,1,128,1024]{2,3,0,1:T(8,128)S(1)} copy(f32[2,1,128,1024]{3,2,1,0:T(8,128)} %param.2) | data formatting | bytes 2097152 | tf_op args[0]
  1.6 0.0 copy-start
  1.6 0.1 copy.13
  1.7 33.1 %all_to_all.33 = f32[2,1,128,4,8,32]{2,5,3,0,1,4:T(8,128)S(1)} all-to-all(f32[2,1,128,4,8,32]{2,5,3,0,1,4:T(8,128)S(1)} %copy.13), channel_id=1, replica_groups=mesh['row'=4,'col'=8] {'col'}, dimensions={4} | all-to-all | bytes 2097152 | tf_op jit(solution)/shard_map/all_to_all | solution.py:19
  34.8 0.6 copy.14
  35.4 0.2 copy.15
  35.6 17.0 %all_to_all.34 = f32[2,1,1024,4,1,32]{2,5,0,4,1,3:T(8,128)S(1)} all-to-all(f32[2,1,1024,4,1,32]{2,5,0,4,1,3:T(8,128)S(1)} %copy.15), channel_id=1, replica_groups=mesh['row'=4,'col'=8] {'row'}, dimensions={3} | all-to-all | bytes 2097152 | tf_op jit(solution)/shard_map/all_to_all | solution.py:20
  52.6 0.1 copy.19
  52.7 0.1 fusion.12
  52.8 0.0 copy-done
  52.8 2.4 %fusion = f32[1024,128]{0,1:S(1)} fusion(f32[1024,128]{0,1:T(8,128)S(1)} %bitcast.59, f32[2,1024,1024]{2,1,0:T(8,128)S(1)} %copy-done), kind=kOutput, calls=%fused_computation | convolution fusion | flops 1610612736 | bytes 5242880
  55.2 2.4 %fusion.6 = f32[1024,128]{0,1:S(1)} fusion(f32[1024,128]{0,1:T(8,128)S(1)} %bitcast.60, f32[2,1024,1024]{2,1,0:T(8,128)S(1)} %copy-done), kind=kOutput, calls=%fused_computation.6 | convolution fusion | flops 1610612736 | bytes 5242880
  57.7 2.4 %fusion.4 = f32[1024,128]{0,1:S(1)} fusion(f32[1024,128]{0,1:T(8,128)S(1)} %bitcast.57, f32[2,1024,1024]{2,1,0:T(8,128)S(1)} %copy-done), kind=kOutput, calls=%fused_computation.4 | convolution fusion | flops 1610612736 | bytes 5242880
  60.1 2.4 %fusion.2 = f32[1024,128]{0,1:S(1)} fusion(f32[1024,128]{0,1:T(8,128)S(1)} %bitcast.58, f32[2,1024,1024]{2,1,0:T(8,128)S(1)} %copy-done), kind=kOutput, calls=%fused_computation.2 | convolution fusion | flops 1610612736 | bytes 5242880
  62.6 0.1 add_bitcast_fusion
  62.7 0.1 maximum_bitcast_fusion
  62.8 1.7 %copy.17 = f32[2,32,4,1024]{3,2,1,0:T(4,128)} copy(f32[2,32,4,1024]{3,1,2,0:T(8,128)S(1)} %maximum_bitcast_fusion) | data formatting | bytes 2097152 | tf_op jit(solution)/shard_map/reshape | solution.py:31
Async XLA Ops:
  1.6 51.2 %copy-start = (f32[2,1024,1024]{2,1,0:T(8,128)S(1)}, f32[2,1024,1024]{2,1,0:T(8,128)}, u32[]{:S(2)}) copy-start(f32[2,1024,1024]{2,1,0:T(8,128)} %param.3) | copy-start | bytes 25165828
where the time goes:
time: 64.7 us; the launch traced here: 64.5 us
  blocking collectives  50.1 us (77%)
  matrix products  9.75 us (15%)
  local copies, waits for them, and re-layouts  4.27 us (7%)
    all_to_all x1, blocking collectives, per_device(): lax.all_to_all(blocks, 'col', split_axis=4, concat_axis=2, tiled=True)  33.1 us
    all_to_all x1, blocking collectives, per_device(): lax.all_to_all(moved, 'row', split_axis=3, concat_axis=1, tiled=True)  17 us
    unnamed x4, matrix products  9.75 us
    reshape x1, local copies, waits for them, and re-layouts, per_device(): return joined.reshape(2, owned, rows_count, middle * opened)  1.65 us
    unnamed x3, local copies, waits for them, and re-layouts  1.55 us

commit v1 on v0

v1 whole, which is shorter than its diff:
```python
import functools

import jax
import jax.numpy as jnp
from jax import lax
from jax.experimental import pallas as pl
from jax.experimental.pallas import tpu as pltpu
from jax.sharding import PartitionSpec as P

LANES = 128
SUBLANES = 8


def plain(stem, branch):
    rows_count = lax.axis_size("row")
    cols_count = lax.axis_size("col")
    entries = stem.shape[2]
    remain = stem.shape[3]
    contract = branch.shape[1]
    opened = branch.shape[2]
    middle = entries * cols_count // contract
    owned = remain // (rows_count * cols_count)
    blocks = stem.reshape(2, 1, entries, rows_count * cols_count, owned)
    blocks = jnp.moveaxis(blocks, 3, 0)
    moved = lax.all_to_all(blocks, ("row", "col"), 0, 0, tiled=True)
    moved = moved.reshape(rows_count, cols_count, 2, entries, owned)
    split = moved.transpose(2, 0, 1, 3, 4).reshape(
        2, rows_count, contract, middle, owned
    )
    high = lax.Precision.HIGHEST
    dot = functools.partial(jnp.einsum, "akml,ko->lamo", precision=high)
    real = dot(split[0], branch[0]) - dot(split[1], branch[1])
    imag = dot(split[0], branch[1]) + dot(split[1], branch[0])
    return jnp.stack([real, imag]).reshape(2, owned, rows_count, middle * opened)


def pack_kernel(stem_ref, out_ref):
    blocks, _, owned, entries = out_ref.shape
    for c in range(2):
        turned = stem_ref[c, 0].T
        out_ref[:, c] = turned.reshape(blocks, owned, entries)


def pack(stem, owned, steps):
    _, _, entries, remain = stem.shape
    width = remain // steps
    return pl.pallas_call(
        pack_kernel,
        grid=(steps,),
        in_specs=[pl.BlockSpec((2, 1, entries, width), lambda i: (0, 0, 0, i))],
        out_specs=pl.BlockSpec(
            (width // owned, 2, owned, entries), lambda i: (i, 0, 0, 0)
        ),
        out_shape=jax.ShapeDtypeStruct(
            (remain // owned, 2, owned, entries), jnp.float32
        ),
        name="pack",
    )(stem)


def halves(x):
    high = x.astype(jnp.bfloat16)
    low = (x - high.astype(jnp.float32)).astype(jnp.bfloat16)
    return high, low


def absorb_kernel(rows_count, moved_ref, branch_ref, out_ref, gathered, high, low):
    blocks, _, owned, entries = moved_ref.shape
    cols_count = blocks // rows_count
    rows = rows_count * owned

    @pl.when(pl.program_id(0) == 0)
    def _():
        for c in range(2):
            for j in range(cols_count):
                for a in range(rows_count):
                    gathered[pl.ds(c * rows + a, owned, stride=rows_count), :] = (
                        moved_ref[a * cols_count + j, c]
                    )
                at = pl.ds(c * rows, rows)
                cols = pl.ds(j * entries, entries)
                high[at, cols], low[at, cols] = halves(gathered[at, :])

    dot = functools.partial(jnp.dot, preferred_element_type=jnp.float32)

    def product(part):
        branch_high, branch_low = halves(branch_ref[part])
        return (
            dot(high[...], branch_low) + dot(low[...], branch_high)
        ) + dot(high[...], branch_high)

    with_real = product(0)
    with_imag = product(1)
    width = out_ref.shape[-1]
    real = with_real[:rows] - with_imag[rows:]
    imag = with_imag[:rows] + with_real[rows:]
    out_ref[0] = real.reshape(owned, rows_count, width)
    out_ref[1] = imag.reshape(owned, rows_count, width)


def absorb(moved, branch, rows_count, steps):
    blocks, _, owned, entries = moved.shape
    _, contract, opened = branch.shape
    width = opened // steps
    rows = 2 * owned * rows_count
    return pl.pallas_call(
        functools.partial(absorb_kernel, rows_count),
        grid=(steps,),
        in_specs=[
            pl.BlockSpec(moved.shape, lambda i: (0, 0, 0, 0)),
            pl.BlockSpec((2, contract, width), lambda i: (0, 0, i)),
        ],
        out_specs=pl.BlockSpec((2, owned, rows_count, width), lambda i: (0, 0, 0, i)),
        out_shape=jax.ShapeDtypeStruct((2, owned, rows_count, opened), jnp.float32),
        scratch_shapes=[
            pltpu.VMEM((rows, entries), jnp.float32),
            pltpu.VMEM((rows, contract), jnp.bfloat16),
            pltpu.VMEM((rows, contract), jnp.bfloat16),
        ],
        name="absorb",
    )(moved, branch)


def per_device(stem, branch):
    rows_count = lax.axis_size("row")
    cols_count = lax.axis_size("col")
    _, _, entries, remain = stem.shape
    _, contract, opened = branch.shape
    owned = remain // (rows_count * cols_count)
    fits = (
        entries * cols_count == contract
        and entries % LANES == 0
        and owned % SUBLANES == 0
        and opened % (4 * LANES) == 0
        and remain % (4 * LANES) == 0
    )
    if not fits:
        return plain(stem, branch)
    packed = pack(stem, owned, 4)
    moved = lax.all_to_all(packed, ("row", "col"), 0, 0, tiled=True)
    return absorb(moved, branch, rows_count, 4)


def solution(mesh):
    placed = (P(None, "row", "col", None), P())
    return jax.shard_map(
        per_device,
        mesh=mesh,
        in_specs=placed,
        out_specs=P(None, ("row", "col"), None, None),
        check_vma=False,
    )
```

time: 64.7 us -> 46.6 us (0.72)
  blocking collectives: 50.1 us -> 34.9 us
  Pallas kernels: 0 us -> 11.4 us
  matrix products: 9.75 us -> 0 us
  local copies, waits for them, and re-layouts: 4.27 us -> 0 us
    all_to_all x2 -> x1, blocking collectives: 50.1 us -> 34.9 us  [per_device(): moved = lax.all_to_all(packed, ('row', 'col'), 0, 0, tiled=True)]
    pallas_call x0 -> x2, Pallas kernels: none -> 11.4 us  [the longest x1 7.82 us: absorb(): pl.pallas_call(functools.partial(absorb_kernel, rows_count), grid=(steps,...]
    unnamed x4 -> x0, matrix products: 9.75 us -> none
    reshape x2 -> x0, local copies, waits for them, and re-layouts: 1.74 us -> none  [the longest x1 1.65 us: per_device(): return joined.reshape(2, owned, rows_count, middle * opened)]
    unnamed x3 -> x0, local copies, waits for them, and re-layouts: 1.55 us -> none
    all_to_all x3 -> x0, local copies, waits for them, and re-layouts: 0.91 us -> none  [the longest x2 0.81 us: per_device(): lax.all_to_all(blocks, 'col', split_axis=4, concat_axis=2, tiled=True)]
where the time goes in v1:
time: 46.6 us; the launch traced here: 46.3 us
  blocking collectives  34.9 us (75%)
  Pallas kernels  11.4 us (24%)
    all_to_all x1, blocking collectives, per_device(): moved = lax.all_to_all(packed, ('row', 'col'), 0, 0, tiled=True)  34.9 us
    pallas_call x1, Pallas kernels, absorb(): pl.pallas_call(functools.partial(absorb_kernel, rows_count), grid=(steps,...  7.82 us
    pallas_call x1, Pallas kernels, pack(): pl.pallas_call(pack_kernel, grid=(steps,), in_specs=[pl.BlockSpec((2, 1,...  3.59 us

profile of v1, /device:TPU:0, one launch (start us, length us, event | category | flops | bytes accessed | tf_op | source)
XLA Modules:
  0.0 46.3 jit_solution(13069346084113954387)
XLA Ops:
  0.0 3.6 %pack.1 = f32[32,2,32,128]{3,2,1,0:T(8,128)} custom-call(f32[2,1,128,1024]{3,2,1,0:T(8,128)} %stem_ref.1), custom_call_target="tpu_custom_call" | custom-call | tf_op jit(solution)/shard_map/pack/pallas_call | solution.py:47
  3.6 34.9 %all_to_all.5.moved_ref = f32[32,2,32,128]{3,2,1,0:T(8,128)} all-to-all(f32[32,2,32,128]{3,2,1,0:T(8,128)} %pack.1), channel_id=1, replica_groups=mesh['row'=4,'col'=8] {'row','col'}, dimensions={0} | all-to-all | bytes 2097152 | tf_op jit(solution)/shard_map/all_to_all | solution.py:140
  38.5 7.8 %absorb.1 = f32[2,32,4,1024]{3,2,1,0:T(4,128)} custom-call(f32[32,2,32,128]{3,2,1,0:T(8,128)} %all_to_all.5.moved_ref, f32[2,1024,1024]{2,1,0:T(8,128)} %branch_ref.1), custom_call_target="tpu_custom_call" | custom-call | tf_op jit(solution)/shard_map/absorb/pallas_call | solution.py:106
